TPU v7x, 32 devices: a whole 2x2x4 slice. The times are simulated.
32 devices in a mesh: dp: 8 (over y, x, core), tensor: 4 (over z).
Axes of the slice: x: 2, y: 2, z: 4, core: 2. Of those that a mesh axis runs over, the one named last changes fastest.
Arguments:
- activations: bfloat16 [8, 1024, 1536], P('dp', 'tensor'), may hold values from -6 to 6
- lengths: int32 [8], P('dp'), may hold values from 256 to 1024, as said below
- attn_gain: bfloat16 [1536], P('dp'), may hold values from 0.5 to 1.5
- w_query: bfloat16 [1536, 1536], P('dp', 'tensor'), may hold values from -0.15625 to 0.15625
- w_key: bfloat16 [1536, 768], P('dp', 'tensor'), may hold values from -0.15625 to 0.15625
- w_value: bfloat16 [1536, 768], P('dp', 'tensor'), may hold values from -0.15625 to 0.15625
- w_out: bfloat16 [1536, 1536], P('tensor', 'dp'), may hold values from -3 to 3
- mlp_gain: bfloat16 [1536], P('dp'), may hold values from 0.5 to 1.5
- w_gate: bfloat16 [1536, 4096], P('dp', 'tensor'), may hold values from -0.15625 to 0.15625
- w_up: bfloat16 [1536, 4096], P('dp', 'tensor'), may hold values from -0.15625 to 0.15625
- w_down: bfloat16 [4096, 1536], P('tensor', 'dp'), may hold values from -0.09375 to 0.09375
- cotangent: bfloat16 [8, 1024, 1536], P('dp', 'tensor'), may hold values from -6 to 6
Outputs:
- out_acts: float32 [8, 1024, 1536], P('dp', 'tensor')
- grad_acts: float32 [8, 1024, 1536], P('dp', 'tensor')
- grad_attn_gain: float32 [1536], P('dp')
- grad_query: float32 [1536, 1536], P('dp', 'tensor')
- grad_key: float32 [1536, 768], P('dp', 'tensor')
- grad_value: float32 [1536, 768], P('dp', 'tensor')
- grad_out: float32 [1536, 1536], P('tensor', 'dp')
- grad_mlp_gain: float32 [1536], P('dp')
- grad_gate: float32 [1536, 4096], P('dp', 'tensor')
- grad_up: float32 [1536, 4096], P('dp', 'tensor')
- grad_down: float32 [4096, 1536], P('tensor', 'dp')
Inputs may be any that keep to these rules, and one draw needn't show every extreme that they name: `lengths`: valid slots of each sequence; in every draw one sequence is full (1024) and one has exactly 256.
All inputs are finite; a program needn't handle non-finite values.
Results may differ from a plain program's by a relative error of at most 0.017.
Values may be sent and summed in bfloat16 or wider, within the bound.
A program may use at most 192 MiB of HBM per device.

v0:
```python
import math

import jax
import jax.numpy as jnp
from jax import lax
from jax.sharding import PartitionSpec as P

HEAD_DIM = 96


EPS = 1e-05
THETA = 100000.0
NEG = -1e30


def rope_tables(count, width):
    half = width // 2
    freqs = THETA ** (-jnp.arange(half, dtype=jnp.float32) * (2.0 / width))
    angles = jnp.arange(count, dtype=jnp.float32)[:, None] * freqs[None, :]
    return (jnp.cos(angles), jnp.sin(angles))


def rotate(vectors, cosines, sines):
    half = vectors.shape[-1] // 2
    first = vectors[..., :half]
    second = vectors[..., half:]
    cos_b = cosines[:, None, :]
    sin_b = sines[:, None, :]
    return jnp.concatenate(
        [first * cos_b - second * sin_b, second * cos_b + first * sin_b], axis=-1
    )


def unrotate(grads, cosines, sines):
    half = grads.shape[-1] // 2
    first = grads[..., :half]
    second = grads[..., half:]
    cos_b = cosines[:, None, :]
    sin_b = sines[:, None, :]
    return jnp.concatenate(
        [first * cos_b + second * sin_b, second * cos_b - first * sin_b], axis=-1
    )


def transposed(left, right):
    return lax.dot_general(
        left, right, (((1,), (1,)), ((), ())), preferred_element_type=jnp.float32
    )


def outer_sum(left, right):
    return lax.dot_general(
        left, right, (((0,), (0,)), ((), ())), preferred_element_type=jnp.float32
    )


def rms_back(grad_norm, normed, inverse):
    return inverse * (grad_norm - normed * jnp.mean(grad_norm * normed, axis=1, keepdims=True))


def scores_block(query_block, key_prefix, start, seq_positions, key_valid, scale):
    block = query_block.shape[0]
    stop = key_prefix.shape[0]
    raw = (
        jnp.einsum("qcgd,kcd->cgqk", query_block, key_prefix, preferred_element_type=jnp.float32)
        * scale
    )
    rows = start + jnp.arange(block)
    allowed = (seq_positions[None, :stop] <= rows[:, None]) & key_valid[None, :stop]
    return jnp.where(allowed, raw, NEG)


def body(
    activations,
    lengths,
    attn_gain,
    w_query,
    w_key,
    w_value,
    w_out,
    mlp_gain,
    w_gate,
    w_up,
    w_down,
    cotangent,
):
    tensor_size = lax.axis_size("tensor")
    tensor_rank = lax.axis_index("tensor")
    tokens = activations[0].astype(jnp.float32)
    local = tokens.shape[0]
    seq_len = local * tensor_size
    length = lengths[0]
    own_valid = (tensor_rank * local + jnp.arange(local) < length)[:, None]
    seq_positions = jnp.arange(seq_len)
    key_valid = seq_positions < length
    cosines, sines = rope_tables(seq_len, HEAD_DIM)
    scale = 1.0 / math.sqrt(HEAD_DIM)
    query_full, key_full, value_full, out_full, first_gain = (
        lax.all_gather(w_query, "dp", axis=0, tiled=True),
        lax.all_gather(w_key, "dp", axis=0, tiled=True),
        lax.all_gather(w_value, "dp", axis=0, tiled=True),
        lax.all_gather(w_out, "dp", axis=1, tiled=True),
        lax.all_gather(attn_gain, "dp", axis=0, tiled=True),
    )
    heads = query_full.shape[1] // HEAD_DIM
    kv_local = key_full.shape[1] // HEAD_DIM
    groups = heads // kv_local
    first_gain_f = first_gain.astype(jnp.float32)
    inv_first = lax.rsqrt(jnp.mean(tokens * tokens, axis=1, keepdims=True) + EPS)
    normed_first = tokens * inv_first
    first_low = (normed_first * first_gain_f).astype(jnp.bfloat16)
    first_all = lax.all_gather(first_low, "tensor", axis=0, tiled=True)
    query_proj = jnp.dot(first_all, query_full, preferred_element_type=jnp.float32).reshape(
        seq_len, heads, HEAD_DIM
    )
    queries = (
        rotate(query_proj, cosines, sines)
        .astype(jnp.bfloat16)
        .reshape(seq_len, kv_local, groups, HEAD_DIM)
    )
    key_proj = jnp.dot(first_all, key_full, preferred_element_type=jnp.float32).reshape(
        seq_len, kv_local, HEAD_DIM
    )
    keys = rotate(key_proj, cosines, sines).astype(jnp.bfloat16)
    values = (
        jnp.dot(first_all, value_full, preferred_element_type=jnp.float32)
        .astype(jnp.bfloat16)
        .reshape(seq_len, kv_local, HEAD_DIM)
    )
    block = min(512, seq_len)
    count = seq_len // block
    pieces = []
    log_sums = []
    for index in range(count):
        start = index * block
        stop = start + block
        scores = scores_block(
            queries[start:stop], keys[:stop], start, seq_positions, key_valid, scale
        )
        peak = jnp.max(scores, axis=3, keepdims=True)
        log_sum = peak + jnp.log(jnp.sum(jnp.exp(scores - peak), axis=3, keepdims=True))
        probs = jnp.exp(scores - log_sum)
        mixed = jnp.einsum(
            "cgqk,kcd->qcgd",
            probs.astype(jnp.bfloat16),
            values[:stop],
            preferred_element_type=jnp.float32,
        )
        pieces.append(mixed.reshape(block, heads * HEAD_DIM))
        log_sums.append(log_sum)
    attended = jnp.concatenate(pieces, axis=0).astype(jnp.bfloat16)
    branch = lax.psum_scatter(
        jnp.dot(attended, out_full, preferred_element_type=jnp.float32),
        "tensor",
        scatter_dimension=0,
        tiled=True,
    )
    middle = tokens + branch
    gate_full, up_full, down_full, second_gain = (
        lax.all_gather(w_gate, "dp", axis=0, tiled=True),
        lax.all_gather(w_up, "dp", axis=0, tiled=True),
        lax.all_gather(w_down, "dp", axis=1, tiled=True),
        lax.all_gather(mlp_gain, "dp", axis=0, tiled=True),
    )
    second_gain_f = second_gain.astype(jnp.float32)
    inv_second = lax.rsqrt(jnp.mean(middle * middle, axis=1, keepdims=True) + EPS)
    normed_second = middle * inv_second
    second_low = (normed_second * second_gain_f).astype(jnp.bfloat16)
    second_all = lax.all_gather(second_low, "tensor", axis=0, tiled=True)
    gate = jnp.dot(second_all, gate_full, preferred_element_type=jnp.float32)
    up_part = jnp.dot(second_all, up_full, preferred_element_type=jnp.float32)
    sigmoid_gate = jax.nn.sigmoid(gate)
    hidden = (gate * sigmoid_gate * up_part).astype(jnp.bfloat16)
    result = middle + lax.psum_scatter(
        jnp.dot(hidden, down_full, preferred_element_type=jnp.float32).astype(jnp.bfloat16),
        "tensor",
        scatter_dimension=0,
        tiled=True,
    ).astype(jnp.float32)
    output = jnp.where(own_valid, result, 0.0)
    query_full, key_full, value_full, out_full, gate_full, up_full, down_full = (
        lax.all_gather(w_query, "dp", axis=0, tiled=True),
        lax.all_gather(w_key, "dp", axis=0, tiled=True),
        lax.all_gather(w_value, "dp", axis=0, tiled=True),
        lax.all_gather(w_out, "dp", axis=1, tiled=True),
        lax.all_gather(w_gate, "dp", axis=0, tiled=True),
        lax.all_gather(w_up, "dp", axis=0, tiled=True),
        lax.all_gather(w_down, "dp", axis=1, tiled=True),
    )
    grad_result = jnp.where(own_valid, cotangent[0].astype(jnp.float32), 0.0)
    grad_mlp_all = lax.all_gather(grad_result.astype(jnp.bfloat16), "tensor", axis=0, tiled=True)
    grad_down_w = outer_sum(hidden, grad_mlp_all)
    grad_hidden = transposed(grad_mlp_all, down_full)
    grad_gate_low = (
        grad_hidden * up_part * sigmoid_gate * (1.0 + gate * (1.0 - sigmoid_gate))
    ).astype(jnp.bfloat16)
    grad_up_low = (grad_hidden * gate * sigmoid_gate).astype(jnp.bfloat16)
    grad_second = lax.psum_scatter(
        transposed(grad_gate_low, gate_full) + transposed(grad_up_low, up_full),
        "tensor",
        scatter_dimension=0,
        tiled=True,
    )
    grad_gate_w = outer_sum(second_all, grad_gate_low)
    grad_up_w = outer_sum(second_all, grad_up_low)
    grad_gate_w, grad_up_w, grad_down_w = (
        lax.psum_scatter(
            grad_gate_w.astype(jnp.bfloat16), "dp", scatter_dimension=0, tiled=True
        ).astype(jnp.float32),
        lax.psum_scatter(
            grad_up_w.astype(jnp.bfloat16), "dp", scatter_dimension=0, tiled=True
        ).astype(jnp.float32),
        lax.psum_scatter(
            grad_down_w.astype(jnp.bfloat16), "dp", scatter_dimension=1, tiled=True
        ).astype(jnp.float32),
    )
    second_gain_part = jnp.sum(grad_second * normed_second, axis=0)
    grad_middle = grad_result + rms_back(grad_second * second_gain_f, normed_second, inv_second)
    grad_attn_all = lax.all_gather(grad_middle.astype(jnp.bfloat16), "tensor", axis=0, tiled=True)
    grad_attended = transposed(grad_attn_all, out_full).astype(jnp.bfloat16)
    grad_out_w = outer_sum(attended, grad_attn_all)
    grad_queries = []
    grad_keys = jnp.zeros((seq_len, kv_local, HEAD_DIM), jnp.float32)
    grad_values = jnp.zeros((seq_len, kv_local, HEAD_DIM), jnp.float32)
    for index in range(count):
        start = index * block
        stop = start + block
        query_block = queries[start:stop]
        scores = scores_block(query_block, keys[:stop], start, seq_positions, key_valid, scale)
        probs = jnp.exp(scores - log_sums[index])
        grad_block = grad_attended[start:stop].reshape(block, kv_local, groups, HEAD_DIM)
        grad_probs = jnp.einsum(
            "qcgd,kcd->cgqk", grad_block, values[:stop], preferred_element_type=jnp.float32
        )
        row_dot = jnp.sum(probs * grad_probs, axis=3, keepdims=True)
        grad_scores = (probs * (grad_probs - row_dot)).astype(jnp.bfloat16)
        query_grad = (
            jnp.einsum(
                "cgqk,kcd->qcgd", grad_scores, keys[:stop], preferred_element_type=jnp.float32
            )
            * scale
        )
        grad_queries.append(query_grad.reshape(block, heads, HEAD_DIM))
        key_grad = (
            jnp.einsum(
                "cgqk,qcgd->kcd", grad_scores, query_block, preferred_element_type=jnp.float32
            )
            * scale
        )
        grad_keys = grad_keys.at[:stop].add(key_grad)
        value_grad = jnp.einsum(
            "cgqk,qcgd->kcd",
            probs.astype(jnp.bfloat16),
            grad_block,
            preferred_element_type=jnp.float32,
        )
        grad_values = grad_values.at[:stop].add(value_grad)
    grad_query_proj = (
        unrotate(jnp.concatenate(grad_queries, axis=0), cosines, sines)
        .astype(jnp.bfloat16)
        .reshape(seq_len, heads * HEAD_DIM)
    )
    grad_key_proj = (
        unrotate(grad_keys, cosines, sines)
        .astype(jnp.bfloat16)
        .reshape(seq_len, kv_local * HEAD_DIM)
    )
    grad_value_proj = grad_values.astype(jnp.bfloat16).reshape(seq_len, kv_local * HEAD_DIM)
    grad_first = lax.psum_scatter(
        (
            transposed(grad_query_proj, query_full)
            + transposed(grad_key_proj, key_full)
            + transposed(grad_value_proj, value_full)
        ).astype(jnp.bfloat16),
        "tensor",
        scatter_dimension=0,
        tiled=True,
    ).astype(jnp.float32)
    grad_query_w = outer_sum(first_all, grad_query_proj)
    grad_key_w = outer_sum(first_all, grad_key_proj)
    grad_value_w = outer_sum(first_all, grad_value_proj)
    grad_query_w, grad_key_w, grad_value_w, grad_out_w = (
        lax.psum_scatter(
            grad_query_w.astype(jnp.bfloat16), "dp", scatter_dimension=0, tiled=True
        ).astype(jnp.float32),
        lax.psum_scatter(
            grad_key_w.astype(jnp.bfloat16), "dp", scatter_dimension=0, tiled=True
        ).astype(jnp.float32),
        lax.psum_scatter(
            grad_value_w.astype(jnp.bfloat16), "dp", scatter_dimension=0, tiled=True
        ).astype(jnp.float32),
        lax.psum_scatter(
            grad_out_w.astype(jnp.bfloat16), "dp", scatter_dimension=1, tiled=True
        ).astype(jnp.float32),
    )
    first_gain_part = jnp.sum(grad_first * normed_first, axis=0)
    grad_tokens = grad_middle + rms_back(grad_first * first_gain_f, normed_first, inv_first)
    first_gain_sum, second_gain_sum = lax.psum(
        (first_gain_part, second_gain_part), ("dp", "tensor")
    )
    width = attn_gain.shape[0]
    dp_rank = lax.axis_index("dp")
    first_gain_grad = lax.dynamic_slice_in_dim(first_gain_sum, dp_rank * width, width)
    second_gain_grad = lax.dynamic_slice_in_dim(second_gain_sum, dp_rank * width, width)
    return (
        output[None],
        grad_tokens[None],
        first_gain_grad,
        grad_query_w,
        grad_key_w,
        grad_value_w,
        grad_out_w,
        second_gain_grad,
        grad_gate_w,
        grad_up_w,
        grad_down_w,
    )


def solution(mesh):
    return jax.shard_map(
        body,
        mesh=mesh,
        in_specs=(
            P("dp", "tensor", None),
            P("dp"),
            P("dp"),
            P("dp", "tensor"),
            P("dp", "tensor"),
            P("dp", "tensor"),
            P("tensor", "dp"),
            P("dp"),
            P("dp", "tensor"),
            P("dp", "tensor"),
            P("tensor", "dp"),
            P("dp", "tensor", None),
        ),
        out_specs=(
            P("dp", "tensor", None),
            P("dp", "tensor", None),
            P("dp"),
            P("dp", "tensor"),
            P("dp", "tensor"),
            P("dp", "tensor"),
            P("tensor", "dp"),
            P("dp"),
            P("dp", "tensor"),
            P("dp", "tensor"),
            P("tensor", "dp"),
        ),
        check_vma=False,
    )
```

profile of v0, /device:TPU:0, one launch (start us, length us, event | category | flops | bytes accessed | tf_op | source)
XLA Modules:
  0.0 1172.5 jit_solution(16675903397976520684)
XLA Ops:
  12.3 15.5 %all-reduce.5 = (bf16[1536]{0:T(1024)(128)(2,1)S(1)}, bf16[1536]{0:T(1024)(128)(2,1)S(1)}) all-reduce(bf16[1536]{0:T(1024)(128)(2,1)S(1)} %dynamic-update-slice.10, bf16[1536]{0:T(1024)(128)(2,1)S(1)} %dynamic-update-slice.11), channel_id=1, replica_groups=mesh['dp'=8,'tensor'=4] {'dp'}, use_global_device_ids=true, to_apply=%add.2 | all-reduce | flops 3072 | bytes 12288
  27.8 2.3 fusion.19
  33.5 9.4 all_gather.49
  42.9 10.4 all_gather.48
  53.6 39.4 %all-gather.10.cloned.1.call-done = bf16[1024,1536]{1,0:T(8,128)(2,1)} async-done(((bf16[256,1536]{1,0:T(8,128)(2,1)}), bf16[1024,1536]{1,0:T(8,128)(2,1)}) %all-gather.10.cloned.1.call-update) | async-done | bytes 3145744 | tf_op jit(solution)/shard_map/all_gather | solution.py:112
  93.0 3.2 convolution_convert_fusion.11
  98.4 19.2 %all-gather.12.cloned.1.call-done = bf16[1536,384]{1,0:T(8,128)(2,1)} async-done(((bf16[192,384]{1,0:T(8,128)(2,1)}), bf16[1536,384]{1,0:T(8,128)(2,1)}) %all-gather.12.cloned.1.call-update) | async-done | bytes 1179664 | tf_op jit(solution)/shard_map/all_gather | solution.py:99
  117.5 3.6 fusion.61
  124.2 1.7 fusion.4
  126.0 2.1 exponential_reduce_fusion
  129.5 2.5 convolution_convert_fusion.9
  132.0 11.4 all-gather.14.cloned.1.call-done
  143.4 5.8 fusion.34
  149.8 110.3 %reduce-scatter.12.cloned.1.call-done = f32[256,1536]{1,0:T(8,128)} async-done(((f32[1024,1536]{1,0:T(8,128)}), f32[256,1536]{1,0:T(8,128)}) %reduce-scatter.12.cloned.1.call-update) | async-done | bytes 1572880 | tf_op jit(solution)/shard_map/reduce_scatter | solution.py:152
  260.1 1.7 multiply_reduce_fusion.2
  263.8 2.2 fusion.24
  267.3 27.3 %all-gather.20.cloned.1.call-done = bf16[1536,1024]{1,0:T(8,128)(2,1)} async-done(((bf16[192,1024]{1,0:T(8,128)(2,1)}), bf16[1536,1024]{1,0:T(8,128)(2,1)}) %all-gather.20.cloned.1.call-update) | async-done | bytes 3145744 | tf_op jit(solution)/shard_map/all_gather | solution.py:161
  294.6 65.5 %all-gather.16.cloned.1.call-done = bf16[1024,1536]{1,0:T(8,128)(2,1)} async-done(((bf16[256,1536]{1,0:T(8,128)(2,1)}), bf16[1024,1536]{1,0:T(8,128)(2,1)}) %all-gather.16.cloned.1.call-update) | async-done | bytes 3145744 | tf_op jit(solution)/shard_map/all_gather | solution.py:169
  360.1 8.2 fusion.63
  368.3 24.5 %all-gather.18.cloned.1.call-done = bf16[1536,1024]{1,0:T(8,128)(2,1)} async-done(((bf16[192,1024]{1,0:T(8,128)(2,1)}), bf16[1536,1024]{1,0:T(8,128)(2,1)}) %all-gather.18.cloned.1.call-update) | async-done | bytes 3145744 | tf_op jit(solution)/shard_map/all_gather | solution.py:160
  392.8 8.2 fusion.62
  401.1 57.4 %all-gather.24.cloned.1.call-done = bf16[1024,1536]{1,0:T(8,128)(2,1)} async-done(((bf16[256,1536]{1,0:T(8,128)(2,1)}), bf16[1024,1536]{1,0:T(8,128)(2,1)}) %all-gather.24.cloned.1.call-update) | async-done | bytes 3145744 | tf_op jit(solution)/shard_map/all_gather | solution.py:191
  458.4 32.7 %all-gather.22.cloned.1.call-done = bf16[1024,1536]{0,1:T(8,128)(2,1)} async-done(((bf16[1024,192]{0,1:T(8,128)(2,1)}), bf16[1024,1536]{0,1:T(8,128)(2,1)}) %all-gather.22.cloned.1.call-update) | async-done | bytes 3145744 | tf_op jit(solution)/shard_map/all_gather | solution.py:162
  491.2 11.7 %multiply_convert_fusion = (bf16[1024,1024]{1,0:T(8,128)(2,1)S(1)}, bf16[1024,1024]{1,0:T(8,128)(2,1)S(1)}, bf16[1024,1024]{1,0:T(8,128)(2,1)}) fusion(f32[1024,1024]{1,0:T(8,128)} %fusion.62, f32[1024,1024]{1,0:T(8,128)} %fusion.63, bf16[1024,1536]{1,0:T(8,128)(2,1)} %all-gather.24.cloned.1.call-done, bf16[1024,1536]{0,1:T(8,128)(2,1)} %all-gather.22.cloned.1.call-done), kind=kOutput, calls=%fused_computation.18 | convolution fusion | flops 3238002688 | bytes 20971520 | tf_op jit(solution)/shard_map/dot_general | solution.py:46
  502.9 3.5 fusion.64
  506.4 5.7 convolution_add_fusion
  512.2 7.7 convolution_convert_fusion.3
  519.9 103.1 %reduce-scatter.16.cloned.1.call-done = f32[256,1536]{1,0:T(8,128)} async-done(((f32[1024,1536]{1,0:T(8,128)}), f32[256,1536]{1,0:T(8,128)}) %reduce-scatter.16.cloned.1.call-update) | async-done | bytes 1572880 | tf_op jit(solution)/shard_map/reduce_scatter | solution.py:198
  623.1 1.9 multiply_reduce_fusion
  624.9 61.4 %reduce-scatter.14.cloned.1.call-done = bf16[256,1536]{1,0:T(8,128)(2,1)} async-done(((bf16[1024,1536]{1,0:T(8,128)(2,1)}), bf16[256,1536]{1,0:T(8,128)(2,1)}) %reduce-scatter.14.cloned.1.call-update) | async-done | bytes 786448 | tf_op jit(solution)/shard_map/reduce_scatter | solution.py:174
  686.3 4.4 fusion.57
  690.8 7.6 convolution_convert_fusion
  698.5 8.0 convolution_convert_fusion.1
  706.6 7.7 convolution_convert_fusion.2
  714.6 39.7 %all-gather.26.cloned.1.call-done = bf16[1024,1536]{1,0:T(8,128)(2,1)} async-done(((bf16[256,1536]{1,0:T(8,128)(2,1)}), bf16[1024,1536]{1,0:T(8,128)(2,1)}) %all-gather.26.cloned.1.call-update) | async-done | bytes 3145744 | tf_op jit(solution)/shard_map/all_gather | solution.py:219
  754.3 3.5 convolution_convert_fusion.8
  759.4 2.4 fusion.7
  764.7 2.5 fusion.29
  768.0 1.9 convolution_convert_fusion.6
  770.0 9.5 fusion
  780.0 7.1 fusion.2
  790.9 2.0 convolution_convert_fusion.7
  793.0 5.1 convolution_convert_fusion.4
  799.6 3.0 convolution_multiply_fusion
  804.5 2.9 convolution_convert_fusion.5
  809.0 1.9 fusion.65
  810.8 2.7 add_convert_fusion
  813.6 2.1 convert_element_type.168
  815.7 36.0 %reduce-scatter.30.cloned.1.call-done = bf16[192,1024]{1,0:T(8,128)(2,1)} async-done(((bf16[1536,1024]{1,0:T(8,128)(2,1)}), bf16[192,1024]{1,0:T(8,128)(2,1)}) %reduce-scatter.30.cloned.1.call-update) | async-done | bytes 393232 | tf_op jit(solution)/shard_map/reduce_scatter | solution.py:210
  851.8 2.0 convert_element_type.166
  853.7 47.4 %reduce-scatter.28.cloned.1.call-done = bf16[192,1024]{1,0:T(8,128)(2,1)} async-done(((bf16[1536,1024]{1,0:T(8,128)(2,1)}), bf16[192,1024]{1,0:T(8,128)(2,1)}) %reduce-scatter.28.cloned.1.call-update) | async-done | bytes 393232 | tf_op jit(solution)/shard_map/reduce_scatter | solution.py:207
  901.1 2.0 convert_element_type.164
  903.1 36.0 %reduce-scatter.24.cloned.1.call-done = bf16[192,192]{1,0:T(8,128)(2,1)} async-done(((bf16[1536,192]{1,0:T(8,128)(2,1)}), bf16[192,192]{1,0:T(8,128)(2,1)}) %reduce-scatter.24.cloned.1.call-update) | async-done | bytes 73744 | tf_op jit(solution)/shard_map/reduce_scatter | solution.py:289
  939.1 1.6 convert_element_type.160
  940.7 36.4 %reduce-scatter.22.cloned.1.call-done = bf16[192,192]{1,0:T(8,128)(2,1)} async-done(((bf16[1536,192]{1,0:T(8,128)(2,1)}), bf16[192,192]{1,0:T(8,128)(2,1)}) %reduce-scatter.22.cloned.1.call-update) | async-done | bytes 73744 | tf_op jit(solution)/shard_map/reduce_scatter | solution.py:286
  977.1 1.6 convert_element_type.158
  978.6 38.2 %reduce-scatter.26.cloned.1.call-done = bf16[384,192]{0,1:T(8,128)(2,1)} async-done(((bf16[384,1536]{0,1:T(8,128)(2,1)}), bf16[384,192]{0,1:T(8,128)(2,1)}) %reduce-scatter.26.cloned.1.call-update) | async-done | bytes 147472 | tf_op jit(solution)/shard_map/reduce_scatter | solution.py:292
  1016.9 1.6 convert_element_type.162
  1018.5 38.3 %reduce-scatter.20.cloned.1.call-done = bf16[192,384]{1,0:T(8,128)(2,1)} async-done(((bf16[1536,384]{1,0:T(8,128)(2,1)}), bf16[192,384]{1,0:T(8,128)(2,1)}) %reduce-scatter.20.cloned.1.call-update) | async-done | bytes 147472 | tf_op jit(solution)/shard_map/reduce_scatter | solution.py:283
  1056.8 1.6 convert_element_type.156
  1058.5 60.9 %reduce-scatter.18.cloned.1.call-done = bf16[256,1536]{1,0:T(8,128)(2,1)} async-done(((bf16[1024,1536]{1,0:T(8,128)(2,1)}), bf16[256,1536]{1,0:T(8,128)(2,1)}) %reduce-scatter.18.cloned.1.call-update) | async-done | bytes 786448 | tf_op jit(solution)/shard_map/reduce_scatter | solution.py:269
  1119.4 1.8 fusion.21
  1121.2 40.3 %all-reduce.4 = (f32[1536]{0:T(1024)S(1)}, f32[1536]{0:T(1024)S(1)}) all-reduce(f32[1536]{0:T(1024)S(1)} %get-tuple-element.77, f32[1536]{0:T(1024)S(1)} %get-tuple-element.75), channel_id=1, replica_groups=mesh['dp'=8,'tensor'=4] {'dp','tensor'}, use_global_device_ids=true, to_apply=%region_15.16 | all-reduce | flops 3072 | bytes 24576 | tf_op jit(solution)/shard_map/psum | solution.py:298
  1162.8 2.7 fusion.18
  (192 shorter events, 33.8 us)
Async XLA Ops:
  7.2 26.4 %copy-start.42 = (bf16[192,192]{1,0:T(8,128)(2,1)S(1)}, bf16[192,192]{1,0:T(8,128)(2,1)}, u32[]{:S(2)}) copy-start(bf16[192,192]{1,0:T(8,128)(2,1)} %param.28) | copy-start | bytes 221188
  7.2 35.7 %copy-start.43 = (bf16[192,192]{1,0:T(8,128)(2,1)S(1)}, bf16[192,192]{1,0:T(8,128)(2,1)}, u32[]{:S(2)}) copy-start(bf16[192,192]{1,0:T(8,128)(2,1)} %param.29) | copy-start | bytes 221188
  7.2 85.8 %all-gather.10.cloned.1.call-start = ((), (), s32[]{:S(2)}) async-start(), calls=%async_computation.11 | async-start | bytes 3932160 | tf_op jit(solution)/shard_map/all_gather | solution.py:112
  8.7 24.9 %copy-start.44 = (f32[256]{0:T(256)}, f32[256]{0:T(256)S(1)}, u32[]{:S(2)}) copy-start(f32[256]{0:T(256)S(1)} %add_rsqrt_fusion.1) | copy-start | bytes 3076
  27.8 5.8 copy-start.40
  30.1 87.4 %all-gather.12.cloned.1.call-start = ((), (), s32[]{:S(2)}) async-start(), calls=%async_computation.12 | async-start | bytes 1327104 | tf_op jit(solution)/shard_map/all_gather | solution.py:99
  30.8 112.5 %all-gather.14.cloned.1.call-start = ((), (), s32[]{:S(2)}) async-start(), calls=%async_computation.13 | async-start | bytes 1327104 | tf_op jit(solution)/shard_map/all_gather | solution.py:102
  31.6 228.6 %reduce-scatter.12.cloned.1.call-start = ((), (), s32[]{:S(2)}) async-start(), calls=%async_computation.14 | async-start | bytes 7864320 | tf_op jit(solution)/shard_map/reduce_scatter | solution.py:152
  33.1 88.1 %copy-start.16 = (f32[1024,48]{0,1:T(8,128)}, f32[1024,48]{0,1:T(8,128)S(1)}, u32[]{:S(2)}) copy-start(f32[1024,48]{0,1:T(8,128)S(1)} %get-tuple-element.103) | copy-start | bytes 589828
  33.1 88.1 %copy-start.18 = (f32[1024,48]{0,1:T(8,128)}, f32[1024,48]{0,1:T(8,128)S(1)}, u32[]{:S(2)}) copy-start(f32[1024,48]{0,1:T(8,128)S(1)} %get-tuple-element.104) | copy-start | bytes 589828
  42.9 55.3 %copy-start.11 = (bf16[1536,192]{1,0:T(8,128)(2,1)}, bf16[1536,192]{1,0:T(8,128)(2,1)S(1)}, u32[]{:S(2)}) copy-start(bf16[1536,192]{1,0:T(8,128)(2,1)S(1)} %all_gather.49) | copy-start | bytes 1769476
  53.3 44.9 %copy-start.9 = (bf16[1536,192]{1,0:T(8,128)(2,1)}, bf16[1536,192]{1,0:T(8,128)(2,1)S(1)}, u32[]{:S(2)}) copy-start(bf16[1536,192]{1,0:T(8,128)(2,1)S(1)} %all_gather.48) | copy-start | bytes 1769476
  53.6 704.3 %copy-start.13 = (pred[512,512]{0,1:T(8,128)(4,1)}, pred[512,512]{0,1:T(8,128)(4,1)S(1)}, u32[]{:S(2)}) copy-start(pred[512,512]{0,1:T(8,128)(4,1)S(1)} %fusion.32) | copy-start | bytes 786436
  93.0 4.0 copy-start.5
  96.3 33.2 %copy-start.20 = (bf16[1024,192]{0,1:T(8,128)(2,1)}, bf16[1024,192]{0,1:T(8,128)(2,1)S(1)}, u32[]{:S(2)}) copy-start(bf16[1024,192]{0,1:T(8,128)(2,1)S(1)} %convolution_convert_fusion.11) | copy-start | bytes 1179652
  98.3 25.8 %copy-start.23 = (bf16[1024,2,48]{0,2,1:T(8,128)(2,1)}, bf16[1024,2,48]{0,2,1:T(8,128)(2,1)S(1)}, u32[]{:S(2)}) copy-start(bf16[1024,2,48]{0,2,1:T(8,128)(2,1)S(1)} %get-tuple-element.97) | copy-start | bytes 589828
  98.4 25.8 %copy-start.25 = (bf16[1024,2,48]{0,2,1:T(8,128)(2,1)}, bf16[1024,2,48]{0,2,1:T(8,128)(2,1)S(1)}, u32[]{:S(2)}) copy-start(bf16[1024,2,48]{0,2,1:T(8,128)(2,1)S(1)} %get-tuple-element.98) | copy-start | bytes 589828
  121.5 2.6 copy-start.27
  123.2 4.9 copy-start.1
  125.9 3.6 copy-start
  125.9 2.2 copy-start.35
  129.5 13.9 %copy-start.36 = (bf16[2,96,2,512]{3,1,2,0:T(8,128)(2,1)}, bf16[2,96,2,512]{3,1,2,0:T(8,128)(2,1)S(1)}, u32[]{:S(2)}) copy-start(bf16[2,96,2,512]{3,1,2,0:T(8,128)(2,1)S(1)} %convolution_convert_fusion.10) | copy-start | bytes 1179652
  132.0 17.2 %copy-start.37 = (bf16[2,96,2,512]{3,1,2,0:T(8,128)(2,1)}, bf16[2,96,2,512]{3,1,2,0:T(8,128)(2,1)S(1)}, u32[]{:S(2)}) copy-start(bf16[2,96,2,512]{3,1,2,0:T(8,128)(2,1)S(1)} %convolution_convert_fusion.9) | copy-start | bytes 1179652
  149.2 111.0 %copy-start.4 = (bf16[1,256,1536]{2,1,0:T(8,128)(2,1)S(1)}, bf16[1,256,1536]{2,1,0:T(8,128)(2,1)}, u32[]{:S(2)}) copy-start(bf16[1,256,1536]{2,1,0:T(8,128)(2,1)} %param.24) | copy-start | bytes 2359300
  149.2 145.4 %all-gather.20.cloned.1.call-start = ((), (), s32[]{:S(2)}) async-start(), calls=%async_computation.17 | async-start | bytes 3538944 | tf_op jit(solution)/shard_map/all_gather | solution.py:161
  149.8 210.3 %all-gather.16.cloned.1.call-start = ((), (), s32[]{:S(2)}) async-start(), calls=%async_computation.15 | async-start | bytes 3932160 | tf_op jit(solution)/shard_map/all_gather | solution.py:169
  262.9 129.9 %all-gather.18.cloned.1.call-start = ((), (), s32[]{:S(2)}) async-start(), calls=%async_computation.16 | async-start | bytes 3538944 | tf_op jit(solution)/shard_map/all_gather | solution.py:160
  263.7 194.7 %all-gather.24.cloned.1.call-start = ((), (), s32[]{:S(2)}) async-start(), calls=%async_computation.20 | async-start | bytes 3932160 | tf_op jit(solution)/shard_map/all_gather | solution.py:191
  266.0 225.2 %all-gather.22.cloned.1.call-start = ((), (), s32[]{:S(2)}) async-start(), calls=%async_computation.18 | async-start | bytes 3538944 | tf_op jit(solution)/shard_map/all_gather | solution.py:162
  266.7 356.3 %reduce-scatter.16.cloned.1.call-start = ((), (), s32[]{:S(2)}) async-start(), calls=%async_computation.21 | async-start | bytes 7864320 | tf_op jit(solution)/shard_map/reduce_scatter | solution.py:198
  491.2 11.7 %copy-start.47 = (bf16[1536,1024]{1,0:T(8,128)(2,1)S(1)}, bf16[1536,1024]{1,0:T(8,128)(2,1)}, u32[]{:S(2)}) copy-start(bf16[1536,1024]{1,0:T(8,128)(2,1)} %all-gather.18.cloned.1.call-done) | copy-start | bytes 9437188
  502.9 3.5 copy-start.49
  502.9 3.5 copy-start.48
  502.9 3.5 copy-start.46
  512.1 174.2 %reduce-scatter.14.cloned.1.call-start = ((), (), s32[]{:S(2)}) async-start(), calls=%async_computation.19 | async-start | bytes 3932160 | tf_op jit(solution)/shard_map/reduce_scatter | solution.py:174
  519.9 234.4 %all-gather.26.cloned.1.call-start = ((), (), s32[]{:S(2)}) async-start(), calls=%async_computation.22 | async-start | bytes 3932160 | tf_op jit(solution)/shard_map/all_gather | solution.py:219
  690.8 122.9 %reduce-scatter.32.cloned.1.call-start = ((), (), s32[]{:S(2)}) async-start(), calls=%async_computation.30 | async-start | bytes 3538944 | tf_op jit(solution)/shard_map/reduce_scatter | solution.py:213
  698.5 153.3 %reduce-scatter.30.cloned.1.call-start = ((), (), s32[]{:S(2)}) async-start(), calls=%async_computation.29 | async-start | bytes 3538944 | tf_op jit(solution)/shard_map/reduce_scatter | solution.py:210
  706.6 194.5 %reduce-scatter.28.cloned.1.call-start = ((), (), s32[]{:S(2)}) async-start(), calls=%async_computation.28 | async-start | bytes 3538944 | tf_op jit(solution)/shard_map/reduce_scatter | solution.py:207
  714.3 39.9 %copy-start.34 = (bf16[384,1536]{0,1:T(8,128)(2,1)S(1)}, bf16[384,1536]{0,1:T(8,128)(2,1)}, u32[]{:S(2)}) copy-start(bf16[384,1536]{0,1:T(8,128)(2,1)} %all-gather.14.cloned.1.call-done) | copy-start | bytes 3538948
  714.4 224.7 %reduce-scatter.24.cloned.1.call-start = ((), (), s32[]{:S(2)}) async-start(), calls=%async_computation.26 | async-start | bytes 884736 | tf_op jit(solution)/shard_map/reduce_scatter | solution.py:289
  754.3 3.6 copy-start.2
  757.8 6.9 copy-start.32
  757.8 6.8 slice-start
  759.4 2.5 copy-start.31
  759.4 4.0 copy-start.14
  759.4 5.3 slice-start.1
  764.7 3.3 copy-start.6
  779.5 197.5 %reduce-scatter.22.cloned.1.call-start = ((), (), s32[]{:S(2)}) async-start(), calls=%async_computation.25 | async-start | bytes 884736 | tf_op jit(solution)/shard_map/reduce_scatter | solution.py:286
  780.0 7.1 copy-start.28
  780.0 7.1 copy-start.29
  787.2 2.1 copy-start.3
  787.2 3.7 copy-start.7
  792.9 5.3 copy-start.24
  792.9 223.9 %reduce-scatter.26.cloned.1.call-start = ((), (), s32[]{:S(2)}) async-start(), calls=%async_computation.27 | async-start | bytes 1327104 | tf_op jit(solution)/shard_map/reduce_scatter | solution.py:292
  798.1 258.7 %reduce-scatter.20.cloned.1.call-start = ((), (), s32[]{:S(2)}) async-start(), calls=%async_computation.24 | async-start | bytes 1327104 | tf_op jit(solution)/shard_map/reduce_scatter | solution.py:283
  802.7 1.9 copy-start.8
  804.5 3.1 copy-start.12
  804.5 3.1 copy-start.22
  807.4 312.0 %reduce-scatter.18.cloned.1.call-start = ((), (), s32[]{:S(2)}) async-start(), calls=%async_computation.23 | async-start | bytes 3932160 | tf_op jit(solution)/shard_map/reduce_scatter | solution.py:269
  809.0 1.9 copy-start.39
  813.6 305.8 %copy-start.41 = (f32[1536]{0:T(1024)S(1)}, f32[1536]{0:T(1024)}, u32[]{:S(2)}) copy-start(f32[1536]{0:T(1024)} %copy-done.40) | copy-start | bytes 18436
  813.6 305.8 %copy-start.45 = (f32[256]{0:T(256)S(1)}, f32[256]{0:T(256)}, u32[]{:S(2)}) copy-start(f32[256]{0:T(256)} %copy-done.44) | copy-start | bytes 3076
  813.6 349.2 %copy-start.15 = (f32[256,1536]{1,0:T(8,128)S(1)}, f32[256,1536]{1,0:T(8,128)}, u32[]{:S(2)}) copy-start(f32[256,1536]{1,0:T(8,128)} %get-tuple-element.84) | copy-start | bytes 4718596
  (8 other events, 9.7 us)
Sparse Core Ops, SparseCore 0:
  30.2 62.7 all-gather.9
  94.9 22.5 all-gather.11
  119.4 23.9 all-gather.13
  149.3 110.7 reduce-scatter.11
  261.9 32.6 all-gather.19
  296.6 63.4 all-gather.15
  362.0 30.8 all-gather.17
  395.0 63.4 all-gather.23
  460.3 30.8 all-gather.21
  512.3 110.7 reduce-scatter.15
  625.4 60.8 reduce-scatter.13
  690.9 63.3 all-gather.25
  757.7 44.7 reduce-scatter.31
  805.7 46.0 reduce-scatter.29
  855.0 46.0 reduce-scatter.27
  904.1 34.9 reduce-scatter.23
  942.1 34.9 reduce-scatter.21
  980.1 36.6 reduce-scatter.25
  1020.1 36.6 reduce-scatter.19
  1059.0 60.3 reduce-scatter.17
where the time goes:
time: 1180 us; the launch traced here: 1170 us
  waiting for transfers between devices  889 us (75%)
  matrix products  132 us (11%)
  blocking collectives  75.5 us (6%)
  other arithmetic  46.9 us (4%)
  between operations  16.7 us (1%)
    reduce_scatter x1, waiting for transfers between devices, body(): lax.psum_scatter(jnp.dot(attended, out_full, preferred_element_type=jnp.f...  110 us
    reduce_scatter x1, waiting for transfers between devices, body(): lax.psum_scatter(transposed(grad_gate_low, gate_full) + transposed(grad_u...  103 us
    all_gather x1, waiting for transfers between devices, body(): second_all = lax.all_gather(second_low, 'tensor', axis=0, tiled=True)  65.5 us
    reduce_scatter x1, waiting for transfers between devices, body(): lax.psum_scatter(jnp.dot(hidden, down_full, preferred_element_type=jnp.fl...  61.4 us
    reduce_scatter x1, waiting for transfers between devices, body(): lax.psum_scatter((transposed(grad_query_proj, query_full) + transposed(gr...  60.9 us
    all_gather x1, waiting for transfers between devices, body(): lax.all_gather(grad_result.astype(jnp.bfloat16), 'tensor', axis=0, tiled=...  57.4 us
    reduce_scatter x1, waiting for transfers between devices, body(): lax.psum_scatter(grad_gate_w.astype(jnp.bfloat16), 'dp', scatter_dimensio...  47.4 us
    psum x1, blocking collectives, body(): lax.psum((first_gain_part, second_gain_part), ('dp', 'tensor'))  40.3 us
  transfers between devices with their start and end apart: 20, of which 19 were waited for; matrix products, arithmetic and copies ran while one was open for 12% of the time, Pallas kernels for 0%

commit v1 on v0

v1 whole, which is shorter than its diff:
```python
import math

import functools

import jax
import jax.numpy as jnp
from jax import lax
from jax.experimental import pallas as pl
from jax.experimental.pallas import tpu as pltpu
from jax.sharding import PartitionSpec as P

MESH = pl.DeviceIdType.MESH
CHUNKS = 4
BF = jnp.bfloat16
F32 = jnp.float32


def greet_line(me, n):
    barrier = pltpu.get_barrier_semaphore()
    for step in (-1, 1):
        there = (me + step >= 0) & (me + step < n)

        @pl.when(there)
        def _():
            pl.semaphore_signal(
                barrier, inc=1, device_id={"tensor": me + step}, device_id_type=MESH
            )

    near = jnp.where(me > 0, 1, 0) + jnp.where(me < n - 1, 1, 0)
    pl.semaphore_wait(barrier, near)


def block(index, piece, rows):
    size = rows // CHUNKS
    return pl.ds(pl.multiple_of(index * rows + piece * size, size), size)


class Gather:
    def __init__(self, me, n, own, out, send, recv):
        self.me, self.n, self.own, self.out = me, n, own, out
        self.send, self.recv = send, recv
        self.rows = own.shape[0]

    def copy(self, way, index, piece, first=False):
        there = self.out.at[block(index, piece, self.rows)]
        return pltpu.make_async_remote_copy(
            src_ref=self.own.at[block(0, piece, self.rows)] if first else there,
            dst_ref=there,
            send_sem=self.send.at[(way + 1) // 2, index, piece],
            recv_sem=self.recv.at[index, piece],
            device_id={"tensor": self.me + way},
            device_id_type=MESH,
        )

    def goes(self, way):
        return (self.me + way >= 0) & (self.me + way < self.n)

    def pass_on(self, way, index, piece):
        @pl.when((index == self.me) & self.goes(way))
        def _():
            self.copy(way, index, piece, True).start()

        @pl.when(((self.me - index) * way > 0) & (index >= 0) & (index < self.n))
        def _():
            self.copy(way, index, piece).wait_recv()

            @pl.when(self.goes(way))
            def _():
                self.copy(way, index, piece).start()

    def close(self, piece):
        for index in range(self.n):
            for way in (1, -1):

                @pl.when((index == self.me) & self.goes(way))
                def _():
                    self.copy(way, index, piece, True).wait_send()

                @pl.when(((self.me - index) * way > 0) & self.goes(way))
                def _():
                    self.copy(way, index, piece).wait_send()


class Scatter:
    def __init__(self, me, n, part, inbox, send, recv):
        self.me, self.n, self.part, self.inbox = me, n, part, inbox
        self.send, self.recv = send, recv
        self.rows = part.shape[0] // n

    def copy(self, way, owner, piece):
        there = block(owner, piece, self.rows)
        return pltpu.make_async_remote_copy(
            src_ref=self.part.at[there],
            dst_ref=self.inbox.at[(way + 1) // 2, there],
            send_sem=self.send.at[owner, piece],
            recv_sem=self.recv.at[(way + 1) // 2, owner, piece],
            device_id={"tensor": self.me + way},
            device_id_type=MESH,
        )

    def comes(self, way):
        return (self.me - way >= 0) & (self.me - way < self.n)

    def pass_on(self, way, owner, piece):
        @pl.when((owner - self.me) * way > 0)
        def _():
            @pl.when(self.comes(way))
            def _():
                self.copy(way, owner, piece).wait_recv()
                here = block(owner, piece, self.rows)
                self.part[here] = (
                    self.part[here].astype(F32) + self.inbox[(way + 1) // 2, here].astype(F32)
                ).astype(BF)

            self.copy(way, owner, piece).start()

    def finish(self, piece, total):
        here = block(self.me, piece, self.rows)
        there = block(0, piece, self.rows)
        total[there] = self.part[here].astype(F32)
        for way in (1, -1):

            @pl.when(self.comes(way))
            def _():
                self.copy(way, self.me, piece).wait_recv()
                total[there] += self.inbox[(way + 1) // 2, here].astype(F32)

    def close(self, piece):
        for owner in range(self.n):
            for way in (1, -1):

                @pl.when((owner - self.me) * way > 0)
                def _():
                    self.copy(way, owner, piece).wait_send()


def pieces(step):
    lax.fori_loop(0, CHUNKS, lambda piece, carry: (step(piece), carry)[1], 0)


LAG = 1


def both_ways(me, n, steps, act):
    near = jnp.where(2 * me < n, 1, -1)
    count = steps * CHUNKS

    def body(index, carry):
        for way, late in ((near, 0), (-near, LAG)):
            at = index - late

            @pl.when((at >= 0) & (at < count))
            def _():
                act(way, at // CHUNKS, at % CHUNKS)

        return carry

    lax.fori_loop(0, count + LAG, body, 0)


def exchange_kernel(n, gathers, scatters, *refs):
    refs = list(refs)
    own = refs.pop(0) if gathers else None
    source = refs.pop(0) if scatters else None
    out = refs.pop(0) if gathers else None
    total = refs.pop(0) if scatters else None
    me = lax.axis_index("tensor")
    gather = scatter = None
    if gathers:
        local, send, recv = refs[:3]
        refs = refs[3:]
        gather = Gather(me, n, own, out, send, recv)
    if scatters:
        part, inbox, load, send, recv = refs
        scatter = Scatter(me, n, part, inbox, send, recv)
        fetch = pltpu.make_async_copy(source, part, load)
        fetch.start()
    greet_line(me, n)
    if gathers:
        keep = pltpu.make_async_copy(own, out.at[pl.ds(me * own.shape[0], own.shape[0])], local)
        keep.start()
    if scatters:
        fetch.wait()

    def act(way, step, piece):
        if scatters:
            index = jnp.where(way > 0, n - 1 - step, step)

            @pl.when(step < n - 1)
            def _():
                scatter.pass_on(way, index, piece)

        if gathers:
            gather.pass_on(way, me - way * step, piece)

    both_ways(me, n, n if gathers else n - 1, act)
    if scatters:
        pieces(lambda piece: scatter.finish(piece, total))
        pieces(scatter.close)
    if gathers:
        pieces(gather.close)
        keep.wait()


def exchange(number, own=None, part=None):
    n = lax.axis_size("tensor")
    gathers, scatters = own is not None, part is not None
    anywhere = pl.BlockSpec(memory_space=pl.ANY)
    operands, in_specs, out_shape, out_specs, scratch = [], [], [], [], []
    if gathers:
        operands.append(own)
        in_specs.append(anywhere)
        out_shape.append(jax.ShapeDtypeStruct((n * own.shape[0], own.shape[1]), own.dtype))
        out_specs.append(anywhere)
        scratch += [
            pltpu.SemaphoreType.DMA,
            pltpu.SemaphoreType.DMA((2, n, CHUNKS)),
            pltpu.SemaphoreType.DMA((n, CHUNKS)),
        ]
    if scatters:
        operands.append(part)
        in_specs.append(anywhere)
        out_shape.append(jax.ShapeDtypeStruct((part.shape[0] // n, part.shape[1]), F32))
        out_specs.append(pl.BlockSpec(memory_space=pltpu.VMEM))
        scratch += [
            pltpu.VMEM(part.shape, BF),
            pltpu.VMEM((2,) + part.shape, BF),
            pltpu.SemaphoreType.DMA,
            pltpu.SemaphoreType.DMA((n, CHUNKS)),
            pltpu.SemaphoreType.DMA((2, n, CHUNKS)),
        ]
    return pl.pallas_call(
        functools.partial(exchange_kernel, n, gathers, scatters),
        out_shape=out_shape,
        in_specs=in_specs,
        out_specs=out_specs,
        scratch_shapes=scratch,
        compiler_params=pltpu.CompilerParams(collective_id=number, has_side_effects=True),
        name=f"exchange_{number}",
    )(*operands)


def greet_peers(axes):
    barrier = pltpu.get_barrier_semaphore()
    for axis in axes:
        me, n = lax.axis_index(axis), lax.axis_size(axis)

        def greet(step, carry):
            pl.semaphore_signal(
                barrier, inc=1, device_id={axis: lax.rem(me + step, n)}, device_id_type=MESH
            )
            return carry

        lax.fori_loop(1, n, greet, 0)
    pl.semaphore_wait(barrier, sum(lax.axis_size(axis) - 1 for axis in axes))


def to_peers(axis, source, inbox, send, recv):
    me, n = lax.axis_index(axis), lax.axis_size(axis)

    def copy(step, back):
        peer = lax.rem(me + step, n)
        slot = lax.rem(me + n - step, n) if back else me
        return pltpu.make_async_remote_copy(
            src_ref=source(peer),
            dst_ref=inbox.at[slot],
            send_sem=send.at[step],
            recv_sem=recv.at[slot],
            device_id={axis: peer},
            device_id_type=MESH,
        )

    def over(act):
        lax.fori_loop(1, n, lambda step, carry: (act(step), carry)[1], 0)

    over(lambda step: copy(step, False).start())
    over(lambda step: copy(step, True).wait_recv())
    return lambda: over(lambda step: copy(step, False).wait_send())


def gain_gather_kernel(own, out, send, recv):
    greet_peers(("dp",))
    out[lax.axis_index("dp")] = own[...]
    to_peers("dp", lambda peer: own, out, send, recv)()


def gain_gather(number, own):
    n = lax.axis_size("dp")
    inside = pl.BlockSpec(memory_space=pltpu.VMEM)
    whole = pl.pallas_call(
        gain_gather_kernel,
        out_shape=jax.ShapeDtypeStruct((n,) + own.shape, F32),
        in_specs=[inside],
        out_specs=inside,
        scratch_shapes=[pltpu.SemaphoreType.DMA((n,))] * 2,
        compiler_params=pltpu.CompilerParams(collective_id=number, has_side_effects=True),
        name="gain_gather",
    )(own)
    return whole.transpose(1, 0, 2).reshape(own.shape[0], -1)


def gain_sum_kernel(part, out, first, second, half, *sems):
    greet_peers(("dp", "tensor"))
    me, line = lax.axis_index("dp"), lax.axis_index("tensor")
    first[me] = part[me]
    done = to_peers("dp", lambda peer: part.at[peer], first, sems[0], sems[1])
    half[...] = jnp.sum(first[...], axis=0)
    second[line] = half[...]
    done_too = to_peers("tensor", lambda peer: half, second, sems[2], sems[3])
    out[...] = jnp.sum(second[...], axis=0)
    done()
    done_too()


def gain_sum(number, part):
    n, m = lax.axis_size("dp"), lax.axis_size("tensor")
    kinds = part.shape[0]
    cut = part.reshape(kinds, n, -1).transpose(1, 0, 2)
    one = cut.shape[1:]
    inside = pl.BlockSpec(memory_space=pltpu.VMEM)
    return pl.pallas_call(
        gain_sum_kernel,
        out_shape=jax.ShapeDtypeStruct(one, F32),
        in_specs=[inside],
        out_specs=inside,
        scratch_shapes=[
            pltpu.VMEM((n,) + one, F32),
            pltpu.VMEM((m,) + one, F32),
            pltpu.VMEM(one, F32),
        ]
        + [pltpu.SemaphoreType.DMA((n,))] * 2
        + [pltpu.SemaphoreType.DMA((m,))] * 2,
        compiler_params=pltpu.CompilerParams(collective_id=number, has_side_effects=True),
        name="gain_sum",
    )(cut)


HEAD_DIM = 96


EPS = 1e-05
THETA = 100000.0
NEG = -1e30


def rope_tables(count, width):
    half = width // 2
    freqs = THETA ** (-jnp.arange(half, dtype=jnp.float32) * (2.0 / width))
    angles = jnp.arange(count, dtype=jnp.float32)[:, None] * freqs[None, :]
    return (jnp.cos(angles), jnp.sin(angles))


def rotate(vectors, cosines, sines):
    half = vectors.shape[-1] // 2
    first = vectors[..., :half]
    second = vectors[..., half:]
    cos_b = cosines[:, None, :]
    sin_b = sines[:, None, :]
    return jnp.concatenate(
        [first * cos_b - second * sin_b, second * cos_b + first * sin_b], axis=-1
    )


def unrotate(grads, cosines, sines):
    half = grads.shape[-1] // 2
    first = grads[..., :half]
    second = grads[..., half:]
    cos_b = cosines[:, None, :]
    sin_b = sines[:, None, :]
    return jnp.concatenate(
        [first * cos_b + second * sin_b, second * cos_b - first * sin_b], axis=-1
    )


def transposed(left, right):
    return lax.dot_general(
        left, right, (((1,), (1,)), ((), ())), preferred_element_type=jnp.float32
    )


def outer_sum(left, right):
    return lax.dot_general(
        left, right, (((0,), (0,)), ((), ())), preferred_element_type=jnp.float32
    )


def rms_back(grad_norm, normed, inverse):
    return inverse * (grad_norm - normed * jnp.mean(grad_norm * normed, axis=1, keepdims=True))


def scores_block(query_block, key_prefix, start, seq_positions, key_valid, scale):
    block = query_block.shape[0]
    stop = key_prefix.shape[0]
    raw = (
        jnp.einsum("qcgd,kcd->cgqk", query_block, key_prefix, preferred_element_type=jnp.float32)
        * scale
    )
    rows = start + jnp.arange(block)
    allowed = (seq_positions[None, :stop] <= rows[:, None]) & key_valid[None, :stop]
    return jnp.where(allowed, raw, NEG)


def body(
    activations,
    lengths,
    attn_gain,
    w_query,
    w_key,
    w_value,
    w_out,
    mlp_gain,
    w_gate,
    w_up,
    w_down,
    cotangent,
):
    tensor_size = lax.axis_size("tensor")
    tensor_rank = lax.axis_index("tensor")
    tokens = activations[0].astype(jnp.float32)
    local = tokens.shape[0]
    seq_len = local * tensor_size
    length = lengths[0]
    own_valid = (tensor_rank * local + jnp.arange(local) < length)[:, None]
    seq_positions = jnp.arange(seq_len)
    key_valid = seq_positions < length
    cosines, sines = rope_tables(seq_len, HEAD_DIM)
    scale = 1.0 / math.sqrt(HEAD_DIM)
    q_width, kv_width = w_query.shape[1], w_key.shape[1]
    ff_width = w_gate.shape[1]
    attn_all = lax.all_gather(
        jnp.concatenate([w_query, w_key, w_value, w_out.T], axis=1), "dp", axis=0, tiled=True
    )
    mlp_all = lax.all_gather(
        jnp.concatenate([w_gate, w_up, w_down.T], axis=1), "dp", axis=0, tiled=True
    )
    cuts = (q_width, q_width + kv_width, q_width + 2 * kv_width)
    query_full, key_full, value_full, out_full = jnp.split(attn_all, cuts, axis=1)
    gate_full, up_full, down_full = jnp.split(mlp_all, 3, axis=1)
    gains = gain_gather(0, jnp.stack([attn_gain, mlp_gain]).astype(jnp.float32))
    first_gain_f, second_gain_f = gains[:1], gains[1:]
    heads = q_width // HEAD_DIM
    kv_local = kv_width // HEAD_DIM
    groups = heads // kv_local
    inv_first = lax.rsqrt(jnp.mean(tokens * tokens, axis=1, keepdims=True) + EPS)
    normed_first = tokens * inv_first
    first_low = (normed_first * first_gain_f).astype(jnp.bfloat16)
    (first_all,) = exchange(1, own=first_low)
    query_proj = jnp.dot(first_all, query_full, preferred_element_type=jnp.float32).reshape(
        seq_len, heads, HEAD_DIM
    )
    queries = (
        rotate(query_proj, cosines, sines)
        .astype(jnp.bfloat16)
        .reshape(seq_len, kv_local, groups, HEAD_DIM)
    )
    key_proj = jnp.dot(first_all, key_full, preferred_element_type=jnp.float32).reshape(
        seq_len, kv_local, HEAD_DIM
    )
    keys = rotate(key_proj, cosines, sines).astype(jnp.bfloat16)
    values = (
        jnp.dot(first_all, value_full, preferred_element_type=jnp.float32)
        .astype(jnp.bfloat16)
        .reshape(seq_len, kv_local, HEAD_DIM)
    )
    span = min(512, seq_len)
    count = seq_len // span
    pieces = []
    log_sums = []
    for index in range(count):
        start = index * span
        stop = start + span
        scores = scores_block(
            queries[start:stop], keys[:stop], start, seq_positions, key_valid, scale
        )
        peak = jnp.max(scores, axis=3, keepdims=True)
        log_sum = peak + jnp.log(jnp.sum(jnp.exp(scores - peak), axis=3, keepdims=True))
        probs = jnp.exp(scores - log_sum)
        mixed = jnp.einsum(
            "cgqk,kcd->qcgd",
            probs.astype(jnp.bfloat16),
            values[:stop],
            preferred_element_type=jnp.float32,
        )
        pieces.append(mixed.reshape(span, heads * HEAD_DIM))
        log_sums.append(log_sum)
    attended = jnp.concatenate(pieces, axis=0).astype(jnp.bfloat16)
    grad_result = jnp.where(own_valid, cotangent[0].astype(jnp.float32), 0.0)
    grad_mlp_all, branch = exchange(
        2,
        own=grad_result.astype(jnp.bfloat16),
        part=transposed(attended, out_full).astype(jnp.bfloat16),
    )
    middle = tokens + branch
    inv_second = lax.rsqrt(jnp.mean(middle * middle, axis=1, keepdims=True) + EPS)
    normed_second = middle * inv_second
    second_low = (normed_second * second_gain_f).astype(jnp.bfloat16)
    (second_all,) = exchange(3, own=second_low)
    gate = jnp.dot(second_all, gate_full, preferred_element_type=jnp.float32)
    up_part = jnp.dot(second_all, up_full, preferred_element_type=jnp.float32)
    sigmoid_gate = jax.nn.sigmoid(gate)
    hidden = (gate * sigmoid_gate * up_part).astype(jnp.bfloat16)
    grad_hidden = jnp.dot(grad_mlp_all, down_full, preferred_element_type=jnp.float32)
    grad_gate_low = (
        grad_hidden * up_part * sigmoid_gate * (1.0 + gate * (1.0 - sigmoid_gate))
    ).astype(jnp.bfloat16)
    grad_up_low = (grad_hidden * gate * sigmoid_gate).astype(jnp.bfloat16)
    grad_second_part = (
        transposed(grad_gate_low, gate_full) + transposed(grad_up_low, up_full)
    ).astype(jnp.bfloat16)
    result_part = transposed(hidden, down_full).astype(jnp.bfloat16)
    mlp_grads = lax.psum_scatter(
        jnp.concatenate(
            [
                outer_sum(second_all, grad_gate_low).astype(jnp.bfloat16),
                outer_sum(second_all, grad_up_low).astype(jnp.bfloat16),
                outer_sum(grad_mlp_all, hidden).astype(jnp.bfloat16),
            ],
            axis=1,
        ),
        "dp",
        scatter_dimension=0,
        tiled=True,
    )
    (grad_second,) = exchange(4, part=grad_second_part)
    second_gain_part = jnp.sum(grad_second * normed_second, axis=0)
    grad_middle = grad_result + rms_back(grad_second * second_gain_f, normed_second, inv_second)
    grad_attn_all, result_sum = exchange(
        5, own=grad_middle.astype(jnp.bfloat16), part=result_part
    )
    output = jnp.where(own_valid, middle + result_sum, 0.0)
    grad_attended = jnp.dot(
        grad_attn_all, out_full, preferred_element_type=jnp.float32
    ).astype(jnp.bfloat16)
    out_grads = lax.psum_scatter(
        outer_sum(grad_attn_all, attended).astype(jnp.bfloat16),
        "dp",
        scatter_dimension=0,
        tiled=True,
    )
    grad_queries = []
    grad_keys = jnp.zeros((seq_len, kv_local, HEAD_DIM), jnp.float32)
    grad_values = jnp.zeros((seq_len, kv_local, HEAD_DIM), jnp.float32)
    for index in range(count):
        start = index * span
        stop = start + span
        query_block = queries[start:stop]
        scores = scores_block(query_block, keys[:stop], start, seq_positions, key_valid, scale)
        probs = jnp.exp(scores - log_sums[index])
        grad_block = grad_attended[start:stop].reshape(span, kv_local, groups, HEAD_DIM)
        grad_probs = jnp.einsum(
            "qcgd,kcd->cgqk", grad_block, values[:stop], preferred_element_type=jnp.float32
        )
        row_dot = jnp.sum(probs * grad_probs, axis=3, keepdims=True)
        grad_scores = (probs * (grad_probs - row_dot)).astype(jnp.bfloat16)
        query_grad = (
            jnp.einsum(
                "cgqk,kcd->qcgd", grad_scores, keys[:stop], preferred_element_type=jnp.float32
            )
            * scale
        )
        grad_queries.append(query_grad.reshape(span, heads, HEAD_DIM))
        key_grad = (
            jnp.einsum(
                "cgqk,qcgd->kcd", grad_scores, query_block, preferred_element_type=jnp.float32
            )
            * scale
        )
        grad_keys = grad_keys.at[:stop].add(key_grad)
        value_grad = jnp.einsum(
            "cgqk,qcgd->kcd",
            probs.astype(jnp.bfloat16),
            grad_block,
            preferred_element_type=jnp.float32,
        )
        grad_values = grad_values.at[:stop].add(value_grad)
    grad_query_proj = (
        unrotate(jnp.concatenate(grad_queries, axis=0), cosines, sines)
        .astype(jnp.bfloat16)
        .reshape(seq_len, heads * HEAD_DIM)
    )
    grad_key_proj = (
        unrotate(grad_keys, cosines, sines)
        .astype(jnp.bfloat16)
        .reshape(seq_len, kv_local * HEAD_DIM)
    )
    grad_value_proj = grad_values.astype(jnp.bfloat16).reshape(seq_len, kv_local * HEAD_DIM)
    grad_first_part = (
        transposed(grad_query_proj, query_full)
        + transposed(grad_key_proj, key_full)
        + transposed(grad_value_proj, value_full)
    ).astype(jnp.bfloat16)
    attn_grads = lax.psum_scatter(
        jnp.concatenate(
            [
                outer_sum(first_all, grad_query_proj).astype(jnp.bfloat16),
                outer_sum(first_all, grad_key_proj).astype(jnp.bfloat16),
                outer_sum(first_all, grad_value_proj).astype(jnp.bfloat16),
            ],
            axis=1,
        ),
        "dp",
        scatter_dimension=0,
        tiled=True,
    )
    (grad_first,) = exchange(6, part=grad_first_part)
    first_gain_part = jnp.sum(grad_first * normed_first, axis=0)
    grad_tokens = grad_middle + rms_back(grad_first * first_gain_f, normed_first, inv_first)
    gain_grads = gain_sum(7, jnp.stack([first_gain_part, second_gain_part]))
    grad_query_w, grad_key_w, grad_value_w = jnp.split(
        attn_grads.astype(jnp.float32), cuts[:2], axis=1
    )
    grad_gate_w, grad_up_w, grad_down_w = jnp.split(mlp_grads.astype(jnp.float32), 3, axis=1)
    return (
        output[None],
        grad_tokens[None],
        gain_grads[0],
        grad_query_w,
        grad_key_w,
        grad_value_w,
        out_grads.astype(jnp.float32).T,
        gain_grads[1],
        grad_gate_w,
        grad_up_w,
        grad_down_w.T,
    )


def solution(mesh):
    return jax.shard_map(
        body,
        mesh=mesh,
        in_specs=(
            P("dp", "tensor", None),
            P("dp"),
            P("dp"),
            P("dp", "tensor"),
            P("dp", "tensor"),
            P("dp", "tensor"),
            P("tensor", "dp"),
            P("dp"),
            P("dp", "tensor"),
            P("dp", "tensor"),
            P("tensor", "dp"),
            P("dp", "tensor", None),
        ),
        out_specs=(
            P("dp", "tensor", None),
            P("dp", "tensor", None),
            P("dp"),
            P("dp", "tensor"),
            P("dp", "tensor"),
            P("dp", "tensor"),
            P("tensor", "dp"),
            P("dp"),
            P("dp", "tensor"),
            P("dp", "tensor"),
            P("tensor", "dp"),
        ),
        check_vma=False,
    )
```

time: 1180 us -> 646 us (0.55)
  waiting for transfers between devices: 889 us -> 39.8 us
  Pallas kernels: 0 us -> 395 us
  blocking collectives: 75.5 us -> 0 us
  matrix products: 132 us -> 102 us
  local copies, waits for them, and re-layouts: 10.6 us -> 39.5 us
    reduce_scatter x11 -> x1, waiting for transfers between devices: 568 us -> 0.01 us  [body(): lax.psum_scatter(outer_sum(grad_attn_all, attended).astype(jnp.bfloat16),...]
    pallas_call x0 -> x8, Pallas kernels: none -> 395 us  [the longest x6 374 us: exchange(): pl.pallas_call(functools.partial(exchange_kernel, n, gathers, scatters),...]
    all_gather x9 -> x2, waiting for transfers between devices: 317 us -> 0.02 us  [the longest x1 0.02 us: body(): lax.all_gather(jnp.concatenate([w_gate, w_up, w_down.T], axis=1), 'dp', a...]
    psum x1 -> x0, blocking collectives: 40.3 us -> none  [body(): lax.psum((first_gain_part, second_gain_part), ('dp', 'tensor'))]
    unnamed x20 -> x7, waiting for transfers between devices: 3.53 us -> 39.8 us
    unnamed x109 -> x140, local copies, waits for them, and re-layouts: 8.55 us -> 31.7 us
    all_gather x2 -> x0, blocking collectives: 19.8 us -> none  [the longest x1 10.4 us: body(): lax.all_gather(w_value, 'dp', axis=0, tiled=True)]
    unnamed x1 -> x0, blocking collectives: 15.5 us -> none
  transfers between devices with their start and end apart: 20 -> 5, of which waited for: 19 -> 1; matrix products, arithmetic and copies ran while one was open for 12% -> 15% of each run, Pallas kernels for 0% -> 41%
where the time goes in v1:
time: 646 us; the launch traced here: 638 us
  Pallas kernels  395 us (61%)
  matrix products  102 us (16%)
  other arithmetic  45.6 us (7%)
  waiting for transfers between devices  39.8 us (6%)
  local copies, waits for them, and re-layouts  39.5 us (6%)
  between operations  15.9 us (2%)
    pallas_call x6, Pallas kernels, exchange(): pl.pallas_call(functools.partial(exchange_kernel, n, gathers, scatters),...  374 us
    unnamed x7, waiting for transfers between devices  39.8 us
    unnamed x140, local copies, waits for them, and re-layouts  31.7 us
    dot_general x7, matrix products, transposed(): lax.dot_general(left, right, (((1,), (1,)), ((), ())), preferred_element_...  26 us
    dot_general x7, matrix products, outer_sum(): lax.dot_general(left, right, (((0,), (0,)), ((), ())), preferred_element_...  20 us
    pallas_call x1, Pallas kernels, gain_sum(): pl.pallas_call(gain_sum_kernel, out_shape=jax.ShapeDtypeStruct(one, F32),...  13.1 us
  transfers between devices with their start and end apart: 5, of which 1 were waited for; matrix products, arithmetic and copies ran while one was open for 15% of the time, Pallas kernels for 41%

profile of v1, /device:TPU:0, one launch (start us, length us, event | category | flops | bytes accessed | tf_op | source)
XLA Modules:
  0.0 637.7 jit_solution(8265091540263678139)
XLA Ops:
  7.3 2.0 concatenate.44
  9.4 2.3 pad_maximum_fusion.2
  13.0 7.5 %gain_gather.1 = f32[8,2,192]{2,1,0:T(2,128)} custom-call(f32[2,192]{1,0:T(2,128)} %maximum_convert_fusion.own), custom_call_target="tpu_custom_call" | custom-call | tf_op jit(solution)/shard_map/gain_gather/pallas_call | solution.py:290
  23.4 55.2 %exchange_1.1 = bf16[1024,1536]{1,0:T(8,128)(2,1)} custom-call(bf16[256,1536]{1,0:T(8,128)(2,1)} %fusion.25.refs_0_), custom_call_target="tpu_custom_call" | custom-call | tf_op jit(solution)/shard_map/exchange_1/pallas_call | solution.py:232
  79.1 1.5 fusion.64
  81.8 2.4 fusion.34.refs_0_
  84.1 3.7 convolution_convert_fusion.12
  87.9 3.0 fusion.47
  91.2 1.7 copy-done.20
  92.9 1.2 fusion.52
  94.3 1.8 fusion.4
  96.1 2.1 exponential_reduce_fusion
  100.1 1.3 convolution_convert_fusion.11
  101.4 2.3 convolution_convert_fusion.10
  104.5 3.5 convolution_convert_fusion.refs_1_
  108.0 86.5 %exchange_2.1 = (bf16[1024,1536]{1,0:T(8,128)(2,1)}, f32[256,1536]{1,0:T(8,128)}) custom-call(bf16[256,1536]{1,0:T(8,128)(2,1)} %fusion.34.refs_0_, bf16[1024,1536]{1,0:T(8,128)(2,1)} %convolution_convert_fusion.refs_1_), custom_call_target="tpu_custom_call" | custom-call | tf_op jit(solution)/shard_map/exchange_2/pallas_call | solution.py:232
  194.6 1.9 multiply_reduce_fusion.2
  198.7 51.2 %exchange_3.1 = bf16[1024,1536]{1,0:T(8,128)(2,1)} custom-call(bf16[256,1536]{1,0:T(8,128)(2,1)} %multiply_convert_fusion.3.refs_0_), custom_call_target="tpu_custom_call" | custom-call | tf_op jit(solution)/shard_map/exchange_3/pallas_call | solution.py:232
  249.9 6.4 %fusion.11 = f32[1024,1024]{1,0:T(8,128)S(1)} fusion(bf16[1024,1536]{1,0:T(8,128)(2,1)} %exchange_3.1, bf16[1536,3072]{1,0:T(8,128)(2,1)} %all-gather.5.cloned.1.call-done), kind=kOutput, calls=%fused_computation.35 | convolution fusion | flops 3221225472 | bytes 10485760 | tf_op jit(solution)/shard_map/dot_general | solution.py:498
  256.3 5.0 fusion.17
  261.4 8.2 %multiply_convert_fusion = (bf16[1024,1024]{1,0:T(8,128)(2,1)}, bf16[1024,1024]{1,0:T(8,128)(2,1)S(1)}, bf16[1024,1024]{1,0:T(8,128)(2,1)}) fusion(f32[1024,1024]{1,0:T(8,128)S(1)} %fusion.11, f32[1024,1024]{1,0:T(8,128)} %fusion.17, bf16[1024,1536]{1,0:T(8,128)(2,1)S(1)} %copy-done.22, bf16[1536,3072]{1,0:T(8,128)(2,1)S(1)} %copy-done.48), kind=kOutput, calls=%fused_computation.19 | convolution fusion | flops 3238002688 | bytes 20971520 | tf_op jit(solution)/shard_map/dot_general | solution.py:499
  269.6 3.4 fusion.9
  273.0 5.0 add_convert_fusion.1.refs_0_
  278.0 50.4 %exchange_4.1 = f32[256,1536]{1,0:T(8,128)} custom-call(bf16[1024,1536]{1,0:T(8,128)(2,1)} %add_convert_fusion.1.refs_0_), custom_call_target="tpu_custom_call" | custom-call | tf_op jit(solution)/shard_map/exchange_4/pallas_call | solution.py:232
  328.4 2.5 multiply_reduce_fusion
  331.2 3.2 fusion.78
  334.5 6.7 %convolution_convert_fusion.4.refs_1_ = bf16[1024,1536]{1,0:T(8,128)(2,1)} fusion(bf16[1024,1024]{1,0:T(8,128)(2,1)S(1)} %copy-done.62, bf16[1536,3072]{1,0:T(8,128)(2,1)} %all-gather.5.cloned.1.call-done), kind=kOutput, calls=%fused_computation.29 | convolution fusion | flops 3222798336 | bytes 8388608 | tf_op jit(solution)/shard_map/dot_general | solution.py:376
  341.1 83.2 %exchange_5.1 = (bf16[1024,1536]{1,0:T(8,128)(2,1)}, f32[256,1536]{1,0:T(8,128)}) custom-call(bf16[256,1536]{1,0:T(8,128)(2,1)} %get-tuple-element.111.refs_0_, bf16[1024,1536]{1,0:T(8,128)(2,1)} %convolution_convert_fusion.4.refs_1_), custom_call_target="tpu_custom_call" | custom-call | tf_op jit(solution)/shard_map/exchange_5/pallas_call | solution.py:232
  424.3 3.8 convolution_convert_fusion.9
  428.9 1.5 fusion.5
  430.5 1.3 fusion.7
  431.8 1.4 convolution_multiply_fusion.1
  433.2 1.6 fusion.41
  434.7 2.1 convolution_bitcast_fusion.2
  436.8 2.9 convolution_convert_fusion.6
  439.7 5.4 fusion
  445.9 2.8 fusion.2
  448.8 1.7 convolution_multiply_fusion
  450.5 1.4 fusion.37
  452.8 3.3 fusion.39
  457.3 2.1 add_convert_fusion.2
  461.1 1.4 convolution_convert_fusion.5
  462.6 2.5 copy.67
  465.2 6.3 convolution_convert_fusion.1
  471.6 4.0 convolution_convert_fusion.2
  475.6 3.8 convolution_convert_fusion.3
  479.4 4.4 pad_maximum_fusion
  483.9 12.6 %copy.69 = bf16[1536,3072]{1,0:T(8,128)(2,1)} copy(bf16[1536,3072]{0,1:T(8,128)(2,1)} %pad_maximum_fusion) | data formatting | bytes 18874368
  497.5 2.3 fusion.50
  500.0 1.8 fusion.45
  501.9 3.2 add_convert_fusion.refs_0_
  505.1 47.9 %exchange_6.1 = f32[256,1536]{1,0:T(8,128)} custom-call(bf16[1024,1536]{1,0:T(8,128)(2,1)} %add_convert_fusion.refs_0_), custom_call_target="tpu_custom_call" | custom-call | tf_op jit(solution)/shard_map/exchange_6/pallas_call | solution.py:232
  553.1 2.3 fusion.31
  556.0 13.1 %gain_sum.1 = f32[2,192]{1,0:T(2,128)} custom-call(f32[8,2,192]{2,1,0:T(2,128)} %maximum_bitcast_fusion.part), custom_call_target="tpu_custom_call" | custom-call | tf_op jit(solution)/shard_map/gain_sum/pallas_call | solution.py:321
  569.2 1.3 fusion.83
  570.5 4.5 fusion.30
  575.0 1.6 convert_bitcast_fusion
  580.3 39.7 %reduce-scatter.12.cloned.1.call-done = bf16[192,3072]{1,0:T(8,128)(2,1)} async-done(((bf16[1536,3072]{1,0:T(8,128)(2,1)}), bf16[192,3072]{1,0:T(8,128)(2,1)}) %reduce-scatter.12.cloned.1.call-update) | async-done | bytes 1179664
  620.0 1.6 copy.70
  622.7 1.9 convert_element_type.145
  624.6 2.4 copy.48
  627.0 1.2 copy.49
  628.2 1.3 slice_bitcast_fusion
  629.5 1.2 copy.50
  (191 shorter events, 23.2 us)
Async XLA Ops:
  7.2 5.2 copy-start.51
  7.2 5.3 copy-start.52
  7.2 14.3 %copy-start.7 = (bf16[1,256,1536]{2,1,0:T(8,128)(2,1)S(1)}, bf16[1,256,1536]{2,1,0:T(8,128)(2,1)}, u32[]{:S(2)}) copy-start(bf16[1,256,1536]{2,1,0:T(8,128)(2,1)} %param.24) | copy-start | bytes 2359300
  7.2 76.9 %all-gather.3.cloned.1.call-start = ((), (), s32[]{:S(2)}) async-start(), calls=%async_computation.3 | async-start | bytes 3981312 | tf_op jit(solution)/shard_map/all_gather | solution.py:430
  9.3 240.6 %all-gather.5.cloned.1.call-start = ((), (), s32[]{:S(2)}) async-start(), calls=%async_computation.4 | async-start | bytes 10616832 | tf_op jit(solution)/shard_map/all_gather | solution.py:433
  11.7 563.3 %reduce-scatter.8.cloned.1.call-start = ((), (), s32[]{:S(2)}) async-start(), calls=%async_computation.5 | async-start | bytes 1327104 | tf_op jit(solution)/shard_map/reduce_scatter | solution.py:534
  21.5 57.1 %copy-start.42 = (f32[1536]{0:T(1024)}, f32[1536]{0:T(1024)S(1)}, u32[]{:S(2)}) copy-start(f32[1536]{0:T(1024)S(1)} %mul.459) | copy-start | bytes 18436
  78.8 252.1 %copy-start.46 = (pred[256]{0:T(512)(128)(4,1)}, pred[256]{0:T(512)(128)(4,1)S(1)}, u32[]{:S(2)}) copy-start(pred[256]{0:T(512)(128)(4,1)S(1)} %add_compare_fusion) | copy-start | bytes 772
  81.8 6.1 copy-start.1
  87.8 13.6 %copy-start.39 = (bf16[1024,192]{0,1:T(8,128)(2,1)}, bf16[1024,192]{0,1:T(8,128)(2,1)S(1)}, u32[]{:S(2)}) copy-start(bf16[1024,192]{0,1:T(8,128)(2,1)S(1)} %convolution_convert_fusion.12) | copy-start | bytes 1179652
  87.8 12.3 %copy-start.40 = (bf16[512,192]{0,1:T(8,128)(2,1)}, bf16[512,192]{0,1:T(8,128)(2,1)S(1)}, u32[]{:S(2)}) copy-start(bf16[512,192]{0,1:T(8,128)(2,1)S(1)} %slice.182) | copy-start | bytes 589828
  87.8 3.0 copy-start.12
  87.9 3.0 copy-start.14
  90.9 2.1 copy-start.20
  92.9 1.4 copy-start.30
  92.9 5.2 copy-start.33
  92.9 1.4 copy-start.10
  94.3 3.9 copy-start.24
  94.3 3.9 copy-start.27
  96.1 5.3 copy-start
  99.2 2.2 copy-start.5
  101.4 2.4 copy-start.53
  249.9 6.4 %copy-start.48 = (bf16[1536,3072]{1,0:T(8,128)(2,1)S(1)}, bf16[1536,3072]{1,0:T(8,128)(2,1)}, u32[]{:S(2)}) copy-start(bf16[1536,3072]{1,0:T(8,128)(2,1)} %all-gather.5.cloned.1.call-done) | copy-start | bytes 28311556
  249.9 6.4 %copy-start.49 = (bf16[1024,1536]{1,0:T(8,128)(2,1)S(1)}, bf16[1024,1536]{1,0:T(8,128)(2,1)}, u32[]{:S(2)}) copy-start(bf16[1024,1536]{1,0:T(8,128)(2,1)} %get-tuple-element.80) | copy-start | bytes 9437188
  256.3 5.0 copy-start.22
  269.6 3.5 copy-start.58
  269.6 3.5 copy-start.60
  328.4 2.5 copy-start.3
  328.4 2.8 copy-start.9
  331.2 3.3 copy-start.62
  424.3 4.6 copy-start.6
  424.3 4.6 copy-start.41
  431.8 1.4 copy-start.34
  434.7 2.1 copy-start.50
  434.7 2.1 copy-start.54
  434.7 2.1 copy-start.56
  436.8 2.9 copy-start.35
  439.7 5.5 slice-start
  439.7 6.2 slice-start.1
  439.7 6.2 copy-start.11
  445.9 2.9 copy-start.26
  445.9 2.9 copy-start.29
  448.8 1.7 copy-start.31
  448.8 1.7 copy-start.32
  450.5 1.4 copy-start.13
  450.5 1.4 copy-start.15
  450.5 2.3 copy-start.36
  450.5 2.3 copy-start.57
  456.2 120.5 %reduce-scatter.10.cloned.1.call-start = ((), (), s32[]{:S(2)}) async-start(), calls=%async_computation.6 | async-start | bytes 2654208
  456.2 3.3 copy-start.37
  457.3 3.0 copy-start.16
  459.5 1.6 copy-start.18
  465.2 6.4 %copy-start.23 = (bf16[1024,1536]{1,0:T(8,128)(2,1)S(1)}, bf16[1024,1536]{1,0:T(8,128)(2,1)}, u32[]{:S(2)}) copy-start(bf16[1024,1536]{1,0:T(8,128)(2,1)} %exchange_3.1) | copy-start | bytes 9437188
  465.2 154.8 %reduce-scatter.12.cloned.1.call-start = ((), (), s32[]{:S(2)}) async-start(), calls=%async_computation.7 | async-start | bytes 10616832
  465.2 6.3 copy-start.61
  471.6 4.1 copy-start.59
  497.5 2.3 copy-start.19
  497.5 2.5 copy-start.21
  500.0 1.9 copy-start.38
  505.1 48.0 %copy-start.8 = (bf16[1,256,1536]{2,1,0:T(8,128)(2,1)S(1)}, bf16[1,256,1536]{2,1,0:T(8,128)(2,1)}, u32[]{:S(2)}) copy-start(bf16[1,256,1536]{2,1,0:T(8,128)(2,1)} %param.24) | copy-start | bytes 2359300
  505.1 48.0 %copy-start.43 = (f32[1536]{0:T(1024)S(1)}, f32[1536]{0:T(1024)}, u32[]{:S(2)}) copy-start(f32[1536]{0:T(1024)} %copy-done.42) | copy-start | bytes 18436
  505.1 48.0 %copy-start.45 = (f32[256]{0:T(256)S(1)}, f32[256]{0:T(256)}, u32[]{:S(2)}) copy-start(f32[256]{0:T(256)} %copy-done.44) | copy-start | bytes 3076
  505.1 65.4 %copy-start.4 = (f32[256,1536]{1,0:T(8,128)S(1)}, f32[256,1536]{1,0:T(8,128)}, u32[]{:S(2)}) copy-start(f32[256,1536]{1,0:T(8,128)} %copy-done.2) | copy-start | bytes 4718596
  505.1 65.4 %copy-start.47 = (pred[256]{0:T(512)(128)(4,1)S(1)}, pred[256]{0:T(512)(128)(4,1)}, u32[]{:S(2)}) copy-start(pred[256]{0:T(512)(128)(4,1)} %copy-done.46) | copy-start | bytes 772
  (6 other events, 6.1 us)
Sparse Core Ops, SparseCore 0:
  10.5 36.5 all-gather.2
  49.5 58.6 all-gather.4
  456.3 37.8 reduce-scatter.7
  497.4 42.3 reduce-scatter.9
  543.1 76.8 reduce-scatter.11
